TPU v7x, 32 devices: a whole 2x2x4 slice. The times are simulated.
32 devices in a mesh: rows: 32 (over z, y, x, core).
Axes of the slice: x: 2, y: 2, z: 4, core: 2. Of those that a mesh axis runs over, the one named last changes fastest.
Arguments:
- source: bfloat16 [65536, 128], P('rows'), may hold values from -6 to 6
- target: bfloat16 [65536, 128], P('rows'), may hold values from -6 to 6
- tile_values: bfloat16 [4096, 128, 128], P('rows'), may hold values from -0.25 to 0.25
- tile_rows: int32 [4096], P('rows'), may hold values from 0 to 15
- tile_peers: int32 [4096], P('rows'), may hold values from 0 to 31
- need_list: int32 [32, 32], P('rows'), may hold values from 0 to 15
- tile_count: int32 [32], P('rows'), may hold values from 1 to 128, as said below
Outputs:
- source_embed: bfloat16 [65536, 128], P('rows')
- target_embed: bfloat16 [65536, 128], P('rows')
Inputs may be any that keep to these rules, and one draw needn't show every extreme that they name: `tile_count`: some device has 128 live tiles; tiles in slots at or past the count take no part.
All inputs are finite; a program needn't handle non-finite values.
Results may differ from a plain program's by a relative error of at most 0.0053.
Values may be sent and summed in bfloat16 or wider, within the bound.
A program may use at most 128 MiB of HBM per device.

v0:
```python
import jax
import jax.numpy as jnp
from jax import lax
from jax.sharding import PartitionSpec as P

ITERS = 2


epsilon = 1e-06


def settle(base, update):
    total = base.astype(jnp.float32) + update
    scale = lax.rsqrt(jnp.mean(total * total, axis=-1, keepdims=True) + epsilon)
    return (total * scale).astype(jnp.bfloat16)


def send_source(outgoing):
    return lax.all_to_all(outgoing, "rows", split_axis=0, concat_axis=0, tiled=True)


def send_partial(partial_value):
    return lax.all_to_all(partial_value, "rows", split_axis=0, concat_axis=0, tiled=True)


def shards(source, target, tile_values, tile_rows, tile_peers, need_list, tile_count):
    peers_total = lax.axis_size("rows")
    tile_side = tile_values.shape[1]
    feature_width = source.shape[1]
    row_count = source.shape[0] // tile_side
    tiles_here = tile_values.shape[0]
    group_size = min(16, tiles_here)
    group_count = tiles_here // group_size
    live_count = tile_count[0]
    wanted = need_list.reshape(peers_total, 1)
    send_list = lax.all_to_all(wanted, "rows", split_axis=0, concat_axis=0, tiled=True)[:, 0]
    owner_hot = (send_list[None, :] == jnp.arange(row_count, dtype=jnp.int32)[:, None]).astype(
        jnp.float32
    )

    def fetch_group(position):
        first_tile = position * group_size
        tile_block = lax.dynamic_slice_in_dim(tile_values, first_tile, group_size, 0)
        row_ids = lax.dynamic_slice_in_dim(tile_rows, first_tile, group_size, 0)
        peer_ids = lax.dynamic_slice_in_dim(tile_peers, first_tile, group_size, 0)
        positions = first_tile + jnp.arange(group_size, dtype=jnp.int32)
        live_mask = (positions < live_count).astype(jnp.float32)[:, None, None]
        return (tile_block, row_ids, peer_ids, live_mask)

    def forward_add(running, fetched, position):
        tile_block, row_ids, peer_ids, live_mask = fetch_group(position)
        product = (
            jnp.einsum(
                "tij,tjk->tik", tile_block, fetched[peer_ids], preferred_element_type=jnp.float32
            )
            * live_mask
        )
        return running.at[row_ids].add(product)

    def backward_add(running, target_blocks, position):
        tile_block, row_ids, peer_ids, live_mask = fetch_group(position)
        product = (
            jnp.einsum(
                "tji,tjk->tik",
                tile_block,
                target_blocks[row_ids],
                preferred_element_type=jnp.float32,
            )
            * live_mask
        )
        return running.at[peer_ids].add(product)

    source_now, target_now = (source, target)
    for iteration in range(ITERS):
        source_blocks = source_now.reshape(row_count, tile_side, feature_width)
        target_blocks = target_now.reshape(row_count, tile_side, feature_width)
        outgoing = source_blocks[send_list]
        empty_rows = jnp.zeros((row_count, tile_side, feature_width), jnp.float32)
        empty_peers = jnp.zeros((peers_total, tile_side, feature_width), jnp.float32)
        partial_value = lax.fori_loop(
            0,
            group_count,
            lambda position, running: backward_add(running, target_blocks, position),
            empty_peers,
        )
        returned = send_partial(partial_value)
        fetched = send_source(outgoing)
        gathered = lax.fori_loop(
            0,
            group_count,
            lambda position, running: forward_add(running, fetched, position),
            empty_rows,
        )
        incoming = jnp.dot(
            owner_hot,
            returned.reshape(peers_total, -1),
            precision=lax.Precision.HIGHEST,
            preferred_element_type=jnp.float32,
        )
        source_now = settle(source, gathered.reshape(-1, feature_width))
        target_now = settle(target, incoming.reshape(-1, feature_width))
    return (source_now, target_now)


def solution(mesh):
    return jax.shard_map(
        shards,
        mesh=mesh,
        in_specs=(
            P("rows", None),
            P("rows", None),
            P("rows", None, None),
            P("rows"),
            P("rows"),
            P("rows", None),
            P("rows"),
        ),
        out_specs=(P("rows", None), P("rows", None)),
        check_vma=False,
    )
```

profile of v0, /device:TPU:0, one launch (start us, length us, event | category | flops | bytes accessed | tf_op | source)
XLA Modules:
  0.0 253.0 jit_solution(12802344706717672668)
XLA Ops:
  2.0 7.3 %all-to-all-start = ((s32[32,1,1]{2,1,0:T(1,128)}), s32[32,1,1]{2,1,0:T(1,128)S(1)}, u32[]{:S(2)}, u32[]{:S(2)}) async-start(s32[32,1,1]{2,1,0:T(1,128)} %copy.14), calls=%async_computation | async-start | bytes 32768 | tf_op jit(solution)/shard_map/all_to_all | solution.py:36
  9.3 6.5 %copy.16 = bf16[128,128,128]{1,2,0:T(8,128)(2,1)} copy(bf16[128,128,128]{2,1,0:T(8,128)(2,1)} %param.17) | data formatting | bytes 8388608 | tf_op jit(solution)/shard_map/while | solution.py:80
  17.1 1.7 gather_fusion.4
  18.8 5.3 %all-to-all-start.1 = ((bf16[32,128,128]{2,1,0:T(8,128)(2,1)}), bf16[32,128,128]{2,1,0:T(8,128)(2,1)}, u32[]{:S(2)}, u32[]{:S(2)}) async-start(bf16[32,128,128]{2,1,0:T(8,128)(2,1)} %gather_fusion.4), calls=%async_computation.1 | async-start | bytes 2097152 | tf_op jit(solution)/shard_map/all_to_all | solution.py:19
  25.7 48.7 %while.54 = (s32[]{:T(128)}, f32[32,128,128]{2,1,0:T(8,128)}, s32[128]{0:T(128)S(1)}, bf16[128,128,128]{1,2,0:T(8,128)(2,1)}, s32[128]{0:T(128)S(1)}, /*index=5*...) while((s32[]{:T(128)}, f32[32,128,128]{2,1,0:T(8,128)}, ...), condition=%wide.region_10.0_spmd, body=%wide.region_8.0_spmd.sunk | while | flops 67634328 | bytes 6296299 | solution.py:80
  28.5 3.3 %scatter_fusion.2 = f32[32,128,128]{2,1,0:T(8,128)} fusion(f32[32,128,128]{2,1,0:T(8,128)} %get-tuple-element.810, s32[16]{0:T(128)S(1)} %get-tuple-element.787, f32[16,128,128]{2,1,0:T(8,128)S(1)} %convolution_multiply_fusion.10), kind=kCustom, calls=%fused_computation.8.clone.1 | custom fusion | flops 262144 | bytes 3145792 | tf_op jit(solution)/shard_map/while/body/eval_jaxpr/scatter-add | solution.py:71
  34.5 3.3 %scatter_fusion.2 = f32[32,128,128]{2,1,0:T(8,128)} fusion(f32[32,128,128]{2,1,0:T(8,128)} %get-tuple-element.810, s32[16]{0:T(128)S(1)} %get-tuple-element.787, f32[16,128,128]{2,1,0:T(8,128)S(1)} %convolution_multiply_fusion.10), kind=kCustom, calls=%fused_computation.8.clone.1 | custom fusion | flops 262144 | bytes 3145792 | tf_op jit(solution)/shard_map/while/body/eval_jaxpr/scatter-add | solution.py:71
  40.6 3.3 %scatter_fusion.2 = f32[32,128,128]{2,1,0:T(8,128)} fusion(f32[32,128,128]{2,1,0:T(8,128)} %get-tuple-element.810, s32[16]{0:T(128)S(1)} %get-tuple-element.787, f32[16,128,128]{2,1,0:T(8,128)S(1)} %convolution_multiply_fusion.10), kind=kCustom, calls=%fused_computation.8.clone.1 | custom fusion | flops 262144 | bytes 3145792 | tf_op jit(solution)/shard_map/while/body/eval_jaxpr/scatter-add | solution.py:71
  46.6 3.3 %scatter_fusion.2 = f32[32,128,128]{2,1,0:T(8,128)} fusion(f32[32,128,128]{2,1,0:T(8,128)} %get-tuple-element.810, s32[16]{0:T(128)S(1)} %get-tuple-element.787, f32[16,128,128]{2,1,0:T(8,128)S(1)} %convolution_multiply_fusion.10), kind=kCustom, calls=%fused_computation.8.clone.1 | custom fusion | flops 262144 | bytes 3145792 | tf_op jit(solution)/shard_map/while/body/eval_jaxpr/scatter-add | solution.py:71
  52.7 3.5 %scatter_fusion.2 = f32[32,128,128]{2,1,0:T(8,128)} fusion(f32[32,128,128]{2,1,0:T(8,128)} %get-tuple-element.810, s32[16]{0:T(128)S(1)} %get-tuple-element.787, f32[16,128,128]{2,1,0:T(8,128)S(1)} %convolution_multiply_fusion.10), kind=kCustom, calls=%fused_computation.8.clone.1 | custom fusion | flops 262144 | bytes 3145792 | tf_op jit(solution)/shard_map/while/body/eval_jaxpr/scatter-add | solution.py:71
  58.9 3.3 %scatter_fusion.2 = f32[32,128,128]{2,1,0:T(8,128)} fusion(f32[32,128,128]{2,1,0:T(8,128)} %get-tuple-element.810, s32[16]{0:T(128)S(1)} %get-tuple-element.787, f32[16,128,128]{2,1,0:T(8,128)S(1)} %convolution_multiply_fusion.10), kind=kCustom, calls=%fused_computation.8.clone.1 | custom fusion | flops 262144 | bytes 3145792 | tf_op jit(solution)/shard_map/while/body/eval_jaxpr/scatter-add | solution.py:71
  65.0 3.3 %scatter_fusion.2 = f32[32,128,128]{2,1,0:T(8,128)} fusion(f32[32,128,128]{2,1,0:T(8,128)} %get-tuple-element.810, s32[16]{0:T(128)S(1)} %get-tuple-element.787, f32[16,128,128]{2,1,0:T(8,128)S(1)} %convolution_multiply_fusion.10), kind=kCustom, calls=%fused_computation.8.clone.1 | custom fusion | flops 262144 | bytes 3145792 | tf_op jit(solution)/shard_map/while/body/eval_jaxpr/scatter-add | solution.py:71
  71.0 3.4 %scatter_fusion.2 = f32[32,128,128]{2,1,0:T(8,128)} fusion(f32[32,128,128]{2,1,0:T(8,128)} %get-tuple-element.810, s32[16]{0:T(128)S(1)} %get-tuple-element.787, f32[16,128,128]{2,1,0:T(8,128)S(1)} %convolution_multiply_fusion.10), kind=kCustom, calls=%fused_computation.8.clone.1 | custom fusion | flops 262144 | bytes 3145792 | tf_op jit(solution)/shard_map/while/body/eval_jaxpr/scatter-add | solution.py:71
  74.4 5.9 %all-to-all-start.3 = ((f32[32,128,128]{2,1,0:T(8,128)}), f32[32,128,128]{2,1,0:T(8,128)}, u32[]{:S(2)}, u32[]{:S(2)}) async-start(f32[32,128,128]{2,1,0:T(8,128)} %get-tuple-element.500), calls=%async_computation.3 | async-start | bytes 4194304 | tf_op jit(solution)/shard_map/all_to_all | solution.py:23
  80.5 44.8 %while.52 = (s32[]{:T(128)}, f32[16,128,128]{2,1,0:T(8,128)S(1)}, s32[128]{0:T(128)S(1)}, bf16[128,128,128]{2,1,0:T(8,128)(2,1)}, s32[128]{0:T(128)S(1)}, /*inde...) while((s32[]{:T(128)}, f32[16,128,128]{2,1,0:T(8,128)S(1)}, ...), condition=%wide.region_2.0_spmd, body=%wide.region_0.0_spmd.sunk | while | flops 67634328 | bytes 6296299 | solution.py:88
  80.6 1.9 gather_fusion
  86.2 1.9 gather_fusion
  91.8 1.9 gather_fusion
  97.4 1.9 gather_fusion
  103.0 1.9 gather_fusion
  108.6 1.9 gather_fusion
  114.2 1.9 gather_fusion
  119.8 1.9 gather_fusion
  123.7 1.6 scatter_fusion
  128.3 1.7 gather_fusion.5
  130.1 5.9 %all-to-all-start.2 = ((bf16[32,128,128]{2,1,0:T(8,128)(2,1)}), bf16[32,128,128]{2,1,0:T(8,128)(2,1)}, u32[]{:S(2)}, u32[]{:S(2)}) async-start(bf16[32,128,128]{2,1,0:T(8,128)(2,1)} %gather_fusion.5), calls=%async_computation.2 | async-start | bytes 2097152 | tf_op jit(solution)/shard_map/all_to_all | solution.py:19
  136.0 3.5 %fusion.11 = f32[16,16384]{1,0:T(8,128)S(1)} fusion(f32[4,8,128,128]{3,2,1,0:T(8,128)} %bitcast.10, s32[32]{0:T(128)S(1)} %reduce), kind=kOutput, calls=%fused_computation.41 | convolution fusion | flops 100663808 | bytes 3145856 | tf_op jit(solution)/shard_map/dot_general | solution.py:94
  141.9 48.3 %while.55 = (s32[]{:T(128)}, f32[32,128,128]{2,1,0:T(8,128)}, s32[128]{0:T(128)S(1)}, bf16[128,128,128]{1,2,0:T(8,128)(2,1)}, s32[128]{0:T(128)S(1)}, /*index=5*...) while((s32[]{:T(128)}, f32[32,128,128]{2,1,0:T(8,128)}, ...), condition=%wide.region_14.0_spmd, body=%wide.region_12.14_spmd.sunk | while | flops 67634328 | bytes 6296299 | solution.py:80
  144.6 3.3 %scatter_fusion.3 = f32[32,128,128]{2,1,0:T(8,128)} fusion(f32[32,128,128]{2,1,0:T(8,128)} %get-tuple-element.843, s32[16]{0:T(128)S(1)} %get-tuple-element.796, f32[16,128,128]{2,1,0:T(8,128)S(1)} %convolution_multiply_fusion.11), kind=kCustom, calls=%fused_computation.9.clone.1 | custom fusion | flops 262144 | bytes 3145792 | tf_op jit(solution)/shard_map/while/body/eval_jaxpr/scatter-add | solution.py:71
  150.6 3.3 %scatter_fusion.3 = f32[32,128,128]{2,1,0:T(8,128)} fusion(f32[32,128,128]{2,1,0:T(8,128)} %get-tuple-element.843, s32[16]{0:T(128)S(1)} %get-tuple-element.796, f32[16,128,128]{2,1,0:T(8,128)S(1)} %convolution_multiply_fusion.11), kind=kCustom, calls=%fused_computation.9.clone.1 | custom fusion | flops 262144 | bytes 3145792 | tf_op jit(solution)/shard_map/while/body/eval_jaxpr/scatter-add | solution.py:71
  156.7 3.3 %scatter_fusion.3 = f32[32,128,128]{2,1,0:T(8,128)} fusion(f32[32,128,128]{2,1,0:T(8,128)} %get-tuple-element.843, s32[16]{0:T(128)S(1)} %get-tuple-element.796, f32[16,128,128]{2,1,0:T(8,128)S(1)} %convolution_multiply_fusion.11), kind=kCustom, calls=%fused_computation.9.clone.1 | custom fusion | flops 262144 | bytes 3145792 | tf_op jit(solution)/shard_map/while/body/eval_jaxpr/scatter-add | solution.py:71
  162.8 3.3 %scatter_fusion.3 = f32[32,128,128]{2,1,0:T(8,128)} fusion(f32[32,128,128]{2,1,0:T(8,128)} %get-tuple-element.843, s32[16]{0:T(128)S(1)} %get-tuple-element.796, f32[16,128,128]{2,1,0:T(8,128)S(1)} %convolution_multiply_fusion.11), kind=kCustom, calls=%fused_computation.9.clone.1 | custom fusion | flops 262144 | bytes 3145792 | tf_op jit(solution)/shard_map/while/body/eval_jaxpr/scatter-add | solution.py:71
  168.8 3.2 %scatter_fusion.3 = f32[32,128,128]{2,1,0:T(8,128)} fusion(f32[32,128,128]{2,1,0:T(8,128)} %get-tuple-element.843, s32[16]{0:T(128)S(1)} %get-tuple-element.796, f32[16,128,128]{2,1,0:T(8,128)S(1)} %convolution_multiply_fusion.11), kind=kCustom, calls=%fused_computation.9.clone.1 | custom fusion | flops 262144 | bytes 3145792 | tf_op jit(solution)/shard_map/while/body/eval_jaxpr/scatter-add | solution.py:71
  174.8 3.3 %scatter_fusion.3 = f32[32,128,128]{2,1,0:T(8,128)} fusion(f32[32,128,128]{2,1,0:T(8,128)} %get-tuple-element.843, s32[16]{0:T(128)S(1)} %get-tuple-element.796, f32[16,128,128]{2,1,0:T(8,128)S(1)} %convolution_multiply_fusion.11), kind=kCustom, calls=%fused_computation.9.clone.1 | custom fusion | flops 262144 | bytes 3145792 | tf_op jit(solution)/shard_map/while/body/eval_jaxpr/scatter-add | solution.py:71
  180.9 3.3 %scatter_fusion.3 = f32[32,128,128]{2,1,0:T(8,128)} fusion(f32[32,128,128]{2,1,0:T(8,128)} %get-tuple-element.843, s32[16]{0:T(128)S(1)} %get-tuple-element.796, f32[16,128,128]{2,1,0:T(8,128)S(1)} %convolution_multiply_fusion.11), kind=kCustom, calls=%fused_computation.9.clone.1 | custom fusion | flops 262144 | bytes 3145792 | tf_op jit(solution)/shard_map/while/body/eval_jaxpr/scatter-add | solution.py:71
  186.9 3.3 %scatter_fusion.3 = f32[32,128,128]{2,1,0:T(8,128)} fusion(f32[32,128,128]{2,1,0:T(8,128)} %get-tuple-element.843, s32[16]{0:T(128)S(1)} %get-tuple-element.796, f32[16,128,128]{2,1,0:T(8,128)S(1)} %convolution_multiply_fusion.11), kind=kCustom, calls=%fused_computation.9.clone.1 | custom fusion | flops 262144 | bytes 3145792 | tf_op jit(solution)/shard_map/while/body/eval_jaxpr/scatter-add | solution.py:71
  190.2 6.2 %all-to-all-start.4 = ((f32[32,128,128]{2,1,0:T(8,128)}), f32[32,128,128]{2,1,0:T(8,128)}, u32[]{:S(2)}, u32[]{:S(2)}) async-start(f32[32,128,128]{2,1,0:T(8,128)} %get-tuple-element.501), calls=%async_computation.4 | async-start | bytes 4194304 | tf_op jit(solution)/shard_map/all_to_all | solution.py:23
  196.6 44.8 %while.53 = (s32[]{:T(128)}, f32[16,128,128]{2,1,0:T(8,128)S(1)}, s32[128]{0:T(128)S(1)}, bf16[128,128,128]{2,1,0:T(8,128)(2,1)}, s32[128]{0:T(128)S(1)}, /*inde...) while((s32[]{:T(128)}, f32[16,128,128]{2,1,0:T(8,128)S(1)}, ...), condition=%wide.region_6.0_spmd, body=%wide.region_4.6_spmd.sunk | while | flops 67634328 | bytes 6296299 | solution.py:88
  196.7 1.9 gather_fusion.1
  202.3 1.9 gather_fusion.1
  207.9 1.9 gather_fusion.1
  213.5 1.9 gather_fusion.1
  219.1 1.9 gather_fusion.1
  224.7 1.9 gather_fusion.1
  230.3 1.9 gather_fusion.1
  235.9 1.9 gather_fusion.1
  242.9 2.2 all-to-all-done.4
  245.1 4.5 %fusion.8 = f32[16,16384]{1,0:T(8,128)} fusion(f32[4,8,128,128]{3,2,1,0:T(8,128)} %bitcast.12, s32[32]{0:T(128)S(1)} %reduce), kind=kOutput, calls=%fused_computation.38 | convolution fusion | flops 100663808 | bytes 3145856 | tf_op jit(solution)/shard_map/dot_general | solution.py:94
  (194 shorter events, 115.5 us)
Async XLA Ops:
  2.0 14.4 %all-to-all-start = ((s32[32,1,1]{2,1,0:T(1,128)}), s32[32,1,1]{2,1,0:T(1,128)S(1)}, u32[]{:S(2)}, u32[]{:S(2)}) async-start(s32[32,1,1]{2,1,0:T(1,128)} %copy.14), calls=%async_computation | async-start | bytes 32768 | tf_op jit(solution)/shard_map/all_to_all | solution.py:36
  9.3 7.8 %copy-start.1 = (bf16[2048,128]{1,0:T(8,128)(2,1)S(1)}, bf16[2048,128]{1,0:T(8,128)(2,1)}, u32[]{:S(2)}) copy-start(bf16[2048,128]{1,0:T(8,128)(2,1)} %param.15) | copy-start | bytes 1572868
  18.8 6.9 %copy-start = (bf16[2048,128]{1,0:T(8,128)(2,1)S(1)}, bf16[2048,128]{1,0:T(8,128)(2,1)}, u32[]{:S(2)}) copy-start(bf16[2048,128]{1,0:T(8,128)(2,1)} %param.16) | copy-start | bytes 1572868
  18.8 6.9 %copy-start.3 = (s32[128]{0:T(128)S(1)}, s32[128]{0:T(128)}, u32[]{:S(2)}) copy-start(s32[128]{0:T(128)} %param.19) | copy-start | bytes 1540
  18.8 6.9 %copy-start.4 = (s32[128]{0:T(128)S(1)}, s32[128]{0:T(128)}, u32[]{:S(2)}) copy-start(s32[128]{0:T(128)} %param.18) | copy-start | bytes 1540
  18.8 55.7 %all-to-all-start.1 = ((bf16[32,128,128]{2,1,0:T(8,128)(2,1)}), bf16[32,128,128]{2,1,0:T(8,128)(2,1)}, u32[]{:S(2)}, u32[]{:S(2)}) async-start(bf16[32,128,128]{2,1,0:T(8,128)(2,1)} %gather_fusion.4), calls=%async_computation.1 | async-start | bytes 2097152 | tf_op jit(solution)/shard_map/all_to_all | solution.py:19
  74.4 55.6 %all-to-all-start.3 = ((f32[32,128,128]{2,1,0:T(8,128)}), f32[32,128,128]{2,1,0:T(8,128)}, u32[]{:S(2)}, u32[]{:S(2)}) async-start(f32[32,128,128]{2,1,0:T(8,128)} %get-tuple-element.500), calls=%async_computation.3 | async-start | bytes 4194304 | tf_op jit(solution)/shard_map/all_to_all | solution.py:23
  130.1 60.2 %all-to-all-start.2 = ((bf16[32,128,128]{2,1,0:T(8,128)(2,1)}), bf16[32,128,128]{2,1,0:T(8,128)(2,1)}, u32[]{:S(2)}, u32[]{:S(2)}) async-start(bf16[32,128,128]{2,1,0:T(8,128)(2,1)} %gather_fusion.5), calls=%async_computation.2 | async-start | bytes 2097152 | tf_op jit(solution)/shard_map/all_to_all | solution.py:19
  190.2 54.9 %all-to-all-start.4 = ((f32[32,128,128]{2,1,0:T(8,128)}), f32[32,128,128]{2,1,0:T(8,128)}, u32[]{:S(2)}, u32[]{:S(2)}) async-start(f32[32,128,128]{2,1,0:T(8,128)} %get-tuple-element.501), calls=%async_computation.4 | async-start | bytes 4194304 | tf_op jit(solution)/shard_map/all_to_all | solution.py:23
  249.6 1.8 copy-start.2
where the time goes:
time: 257 us; the launch traced here: 253 us
  other arithmetic  110 us (43%)
  local copies, waits for them, and re-layouts  56.5 us (22%)
  matrix products  50.7 us (20%)
  starting transfers between devices  30.7 us (12%)
  waiting for transfers between devices  2.83 us (1%)
    scatter-add x16, other arithmetic, backward_add(): return running.at[peer_ids].add(product)  53.2 us
    gather x16, local copies, waits for them, and re-layouts, forward_add(): fetched[peer_ids]  30 us
    scatter-add x16, other arithmetic, forward_add(): return running.at[row_ids].add(product)  25.7 us
    dot_general x16, matrix products, backward_add(): jnp.einsum('tji,tjk->tik', tile_block, target_blocks[row_ids], preferred_...  21.4 us
    dot_general x16, matrix products, forward_add(): jnp.einsum('tij,tjk->tik', tile_block, fetched[peer_ids], preferred_eleme...  21.4 us
    convert_element_type x32, other arithmetic, fetch_group(): live_mask = (positions < live_count).astype(jnp.float32)[:, None, None]  20.8 us
    all_to_all x2, starting transfers between devices, send_partial(): lax.all_to_all(partial_value, 'rows', split_axis=0, concat_axis=0, tiled=...  12.1 us
    all_to_all x2, starting transfers between devices, send_source(): lax.all_to_all(outgoing, 'rows', split_axis=0, concat_axis=0, tiled=True)  11.2 us
  transfers between devices with their start and end apart: 5, of which 2 were waited for; matrix products, arithmetic and copies ran while one was open for 81% of the time, Pallas kernels for 0%

commit v1 on v0

v1 whole, which is shorter than its diff:
```python
import functools

import jax
import jax.numpy as jnp
from jax import lax
from jax.experimental import pallas as pl
from jax.experimental.pallas import tpu as pltpu
from jax.sharding import PartitionSpec as P

ITERS = 2
UNROLL = 4
epsilon = 1e-06
MESH = pl.DeviceIdType.MESH


def plan_groups(keys, live, groups, per_slot, slots):
    items = keys.shape[0]
    item = jnp.arange(items, dtype=jnp.int32)
    group = jnp.arange(groups, dtype=jnp.int32)
    slot = jnp.arange(slots, dtype=jnp.int32)
    member = (keys[None, :] == group[:, None]) & live[None, :]
    count = jnp.sum(member.astype(jnp.int32), axis=1)
    used = (count + per_slot - 1) // per_slot
    start = jnp.sum(jnp.where(group[None, :] < group[:, None], used[None, :], 0), axis=1)
    same = (keys[None, :] == keys[:, None]) & live[None, :] & (item[None, :] < item[:, None])
    rank = jnp.sum(same.astype(jnp.int32), axis=1)
    first = jnp.sum(jnp.where(keys[:, None] == group[None, :], start[None, :], 0), axis=1)
    place = jnp.where(live, per_slot * first + rank, -1)
    seat = jnp.arange(slots * per_slot, dtype=jnp.int32)
    hot = place[None, :] == seat[:, None]
    filled = jnp.any(hot, axis=1)
    chosen = jnp.sum(jnp.where(hot, item[None, :], 0), axis=1)
    opens = jnp.any((start[None, :] == slot[:, None]) & (used[None, :] > 0), axis=1)
    keep = 1 - opens.astype(jnp.int32)
    last = jnp.where(used > 0, start + used - 1, slots)
    return hot, filled, chosen, keep, last


def pick(hot, filled, values, otherwise):
    return jnp.where(filled, jnp.sum(jnp.where(hot, values[None, :], 0), axis=1), otherwise)


def slots_for(items, groups):
    pairs = (items + min(items, groups)) // 2
    return -(-pairs // UNROLL) * UNROLL


def kernel(
    n,
    offsets,
    f_slots,
    b_slots,
    meta,
    source,
    target,
    tiles,
    source_out,
    target_out,
    x_out,
    x_ins,
    y_out,
    y_ins,
    x_now,
    y_now,
    y_base,
    f_sums,
    b_sums,
    c_sums,
    send_sem,
    recv_sem,
):
    me = lax.axis_index("rows")
    rows, side, width = source.shape
    o = offsets

    barrier = pltpu.get_barrier_semaphore()

    def greet(k, carry):
        pl.semaphore_signal(
            barrier, inc=1, device_id=(lax.rem(me + k, n),), device_id_type=MESH
        )
        return carry

    lax.fori_loop(1, n, greet, 0)

    zero_block = jnp.zeros((side, width), jnp.bfloat16)
    zero_sum = jnp.zeros((side, width), jnp.float32)
    for it in range(ITERS):
        x_ins[it][n] = zero_block
    y_now[rows] = zero_block
    f_sums[f_slots] = zero_sum
    b_sums[b_slots] = zero_block
    c_sums[n] = zero_sum

    def turn(b, carry):
        flipped = target[b].astype(jnp.float32).T
        y_base[b] = flipped
        y_now[b] = flipped.astype(jnp.bfloat16)
        return carry

    lax.fori_loop(0, rows, turn, 0)

    def send(out, inn, phase, it):
        def one(k, carry):
            peer = lax.rem(me + k, n)
            pltpu.make_async_remote_copy(
                src_ref=out.at[it, peer],
                dst_ref=inn.at[me],
                send_sem=send_sem.at[phase],
                recv_sem=recv_sem.at[phase],
                device_id=(peer,),
                device_id_type=MESH,
            ).start()
            return carry

        lax.fori_loop(1, n, one, 0)
        inn[me] = out[it, me]

    def all_of(buffer, sem):
        view = buffer.at[pl.ds(0, n - 1)]
        pltpu.make_async_copy(view, view, sem).wait()

    def send_x(blocks, it):
        def one(p, carry):
            x_out[it, p] = blocks[meta[o["send"] + p]]
            return carry

        lax.fori_loop(0, n, one, 0)
        send(x_out, x_ins[it], 2 * it, it)

    def backward(it):
        def one(q, total):
            left, right = 2 * q, 2 * q + 1
            flipped = jnp.concatenate(
                [y_now[meta[o["b_row"] + left]], y_now[meta[o["b_row"] + right]]], axis=1
            )
            stack = jnp.concatenate(
                [tiles[meta[o["b_tile"] + left]], tiles[meta[o["b_tile"] + right]]], axis=0
            )
            product = jnp.dot(flipped, stack, preferred_element_type=jnp.float32)
            total = total * meta[o["b_keep"] + q].astype(jnp.float32) + product
            b_sums[q] = total.astype(jnp.bfloat16)
            return total

        lax.fori_loop(0, b_slots, one, zero_sum, unroll=UNROLL)

        def place(p, carry):
            y_out[it, p] = b_sums[meta[o["b_last"] + p]]
            return carry

        lax.fori_loop(0, n, place, 0)
        send(y_out, y_ins[it], 2 * it + 1, it)

    def forward(it, result):
        x_in = x_ins[it]
        all_of(x_in, recv_sem.at[2 * it])

        def one(q, total):
            left, right = 2 * q, 2 * q + 1
            stack = jnp.concatenate(
                [tiles[meta[o["f_tile"] + left]], tiles[meta[o["f_tile"] + right]]], axis=1
            )
            blocks = jnp.concatenate(
                [x_in[meta[o["f_peer"] + left]], x_in[meta[o["f_peer"] + right]]], axis=0
            )
            product = jnp.dot(stack, blocks, preferred_element_type=jnp.float32)
            total = total * meta[o["f_keep"] + q].astype(jnp.float32) + product
            f_sums[q] = total
            return total

        lax.fori_loop(0, f_slots, one, zero_sum, unroll=UNROLL)

        def settle(b, carry):
            total = source[b].astype(jnp.float32) + f_sums[meta[o["f_last"] + b]]
            scale = lax.rsqrt(jnp.mean(total * total, axis=-1, keepdims=True) + epsilon)
            result[b] = (total * scale).astype(jnp.bfloat16)
            return carry

        lax.fori_loop(0, rows, settle, 0)

    def combine(it, final):
        y_in = y_ins[it]
        all_of(y_in, recv_sem.at[2 * it + 1])

        def one(k, total):
            part = y_in[meta[o["c_from"] + k]].astype(jnp.float32)
            total = total * meta[o["c_keep"] + k].astype(jnp.float32) + part
            c_sums[k] = total
            return total

        lax.fori_loop(0, n, one, zero_sum)

        def settle(b, carry):
            total = y_base[b] + c_sums[meta[o["c_last"] + b]]
            scale = lax.rsqrt(jnp.mean(total * total, axis=0, keepdims=True) + epsilon)
            if final:
                target_out[b] = (total * scale).T.astype(jnp.bfloat16)
            else:
                y_now[b] = (total * scale).astype(jnp.bfloat16)
            return carry

        lax.fori_loop(0, rows, settle, 0)

    pl.semaphore_wait(barrier, n - 1)
    send_x(source, 0)
    backward(0)
    for it in range(ITERS):
        final = it == ITERS - 1
        forward(it, source_out if final else x_now)
        if not final:
            send_x(x_now, it + 1)
        combine(it, final)
        if not final:
            backward(it + 1)
    for it in range(ITERS):
        all_of(x_out.at[it], send_sem.at[2 * it])
        all_of(y_out.at[it], send_sem.at[2 * it + 1])


def shards(source, target, tile_values, tile_rows, tile_peers, need_list, tile_count):
    n = lax.axis_size("rows")
    tiles_here, side, _ = tile_values.shape
    width = source.shape[1]
    rows = source.shape[0] // side
    live = jnp.arange(tiles_here, dtype=jnp.int32) < tile_count[0]
    send_list = lax.all_to_all(
        need_list.reshape(n, 1), "rows", split_axis=0, concat_axis=0, tiled=True
    )[:, 0]
    f_slots = slots_for(tiles_here, rows)
    b_slots = slots_for(tiles_here, n)
    f_hot, f_filled, f_tile, f_keep, f_last = plan_groups(tile_rows, live, rows, 2, f_slots)
    b_hot, b_filled, b_tile, b_keep, b_last = plan_groups(tile_peers, live, n, 2, b_slots)
    everyone = jnp.ones((n,), jnp.bool_)
    _, _, c_from, c_keep, c_last = plan_groups(send_list, everyone, rows, 1, n)
    pieces = dict(
        f_tile=f_tile,
        f_peer=pick(f_hot, f_filled, tile_peers, n),
        f_keep=f_keep,
        f_last=f_last,
        b_tile=b_tile,
        b_row=pick(b_hot, b_filled, tile_rows, rows),
        b_keep=b_keep,
        b_last=b_last,
        send=send_list,
        c_from=c_from,
        c_keep=c_keep,
        c_last=c_last,
    )
    offsets, at = {}, 0
    for name, piece in pieces.items():
        offsets[name] = at
        at += piece.shape[0]
    meta = jnp.concatenate(list(pieces.values()))
    block = (side, width)
    vmem = pl.BlockSpec(memory_space=pltpu.VMEM)
    source_now, target_now = pl.pallas_call(
        functools.partial(kernel, n, offsets, f_slots, b_slots),
        out_shape=[jax.ShapeDtypeStruct((rows,) + block, jnp.bfloat16)] * 2,
        in_specs=[pl.BlockSpec(memory_space=pltpu.SMEM), vmem, vmem, vmem],
        out_specs=[vmem, vmem],
        scratch_shapes=[
            pltpu.VMEM((ITERS, n) + block, jnp.bfloat16),
            [pltpu.VMEM((n + 1,) + block, jnp.bfloat16)] * ITERS,
            pltpu.VMEM((ITERS, n) + block, jnp.bfloat16),
            [pltpu.VMEM((n,) + block, jnp.bfloat16)] * ITERS,
            pltpu.VMEM((rows,) + block, jnp.bfloat16),
            pltpu.VMEM((rows + 1,) + block, jnp.bfloat16),
            pltpu.VMEM((rows,) + block, jnp.float32),
            pltpu.VMEM((f_slots + 1,) + block, jnp.float32),
            pltpu.VMEM((b_slots + 1,) + block, jnp.bfloat16),
            pltpu.VMEM((n + 1,) + block, jnp.float32),
            pltpu.SemaphoreType.DMA((2 * ITERS,)),
            pltpu.SemaphoreType.DMA((2 * ITERS,)),
        ],
        compiler_params=pltpu.CompilerParams(
            collective_id=0, has_side_effects=True, vmem_limit_bytes=67043328
        ),
    )(
        meta,
        source.reshape((rows,) + block),
        target.reshape((rows,) + block),
        tile_values,
    )
    return source_now.reshape(-1, width), target_now.reshape(-1, width)


def solution(mesh):
    return jax.shard_map(
        shards,
        mesh=mesh,
        in_specs=(
            P("rows", None),
            P("rows", None),
            P("rows", None, None),
            P("rows"),
            P("rows"),
            P("rows", None),
            P("rows"),
        ),
        out_specs=(P("rows", None), P("rows", None)),
        check_vma=False,
    )
```

time: 257 us -> 125 us (0.49)
  the two profiles are of different devices: /device:TPU:0 before, /device:TPU:13 now
where the time goes in v1:
time: 125 us; the launch traced here: 123 us
  Pallas kernels  102 us (82%)
  other arithmetic  7.68 us (6%)
  starting transfers between devices  6.27 us (5%)
  local copies, waits for them, and re-layouts  5.76 us (5%)
  between operations  1.39 us (1%)
    pallas_call x1, Pallas kernels, shards(): pl.pallas_call(functools.partial(kernel, n, offsets, f_slots, b_slots), o...  102 us
    all_to_all x1, starting transfers between devices, shards(): lax.all_to_all(need_list.reshape(n, 1), 'rows', split_axis=0, concat_axis...  6.27 us
    unnamed x2, local copies, waits for them, and re-layouts  3.74 us
  transfers between devices with their start and end apart: 1, of which 0 were waited for; matrix products, arithmetic and copies ran while one was open for 5% of the time, Pallas kernels for 0%

profile of v1, /device:TPU:13, one launch (start us, length us, event | category | flops | bytes accessed | tf_op | source)
XLA Modules:
  0.0 123.5 jit_solution(17614016260620686793)
XLA Ops:
  0.6 1.3 %copy.11 = s32[32,1,1]{2,1,0:T(1,128)} copy(s32[32,1,1]{0,2,1:T(1,128)} %bitcast.12) | data formatting | bytes 256 | tf_op jit(solution)/shard_map/all_to_all | solution.py:226
  2.0 6.3 %all-to-all-start = ((s32[32,1,1]{2,1,0:T(1,128)}), s32[32,1,1]{2,1,0:T(1,128)S(1)}, u32[]{:S(2)}, u32[]{:S(2)}) async-start(s32[32,1,1]{2,1,0:T(1,128)} %copy.11), calls=%async_computation | async-start | bytes 32768 | tf_op jit(solution)/shard_map/all_to_all | solution.py:226
  8.9 0.8 convert_reduce_fusion.3
  9.7 0.8 convert_reduce_fusion.5
  10.5 0.9 convert_reduce_fusion
  11.4 0.1 select_reduce_fusion.10
  11.5 0.7 select_reduce_fusion.9
  12.3 0.1 select_reduce_fusion.6
  12.4 0.7 select_reduce_fusion.5
  13.2 0.1 fusion.1
  13.3 0.8 select_reduce_fusion.2
  14.1 0.1 fusion
  14.2 0.8 select_reduce_fusion
  15.0 0.1 fusion.10
  15.1 0.1 fusion.7
  15.2 0.0 all-to-all-done
  15.2 0.7 reduce
  15.9 0.1 convert_reduce_fusion.4
  16.0 0.1 select_reduce_fusion.8
  16.2 0.1 select_reduce_fusion.7
  16.3 0.2 convert_reduce_fusion.2
  16.4 0.1 fusion.12
  16.6 0.1 select_reduce_fusion.4
  16.7 0.7 concatenate.3.meta
  17.3 102.4 %shard_map.86 = (bf16[16,128,128]{2,1,0:T(8,128)(2,1)}, bf16[16,128,128]{2,1,0:T(8,128)(2,1)}) custom-call(s32[920]{0:T(1024)} %concatenate.3.meta, bf16[16,128,128]{2,1,0:T(8,128)(2,1)} %bitcast.8, bf16[16,128,128]{2,1,0:T(8,128)(2,1)} %bitcast.9, bf16[128,128,128]{2,1,0:T(8,128)(2,1)} %tiles.1), custom_call_target="tpu_custom_call" | custom-call | tf_op jit(solution)/shard_map/pallas_call | solution.py:256
  119.7 1.9 %copy.15 = bf16[2048,128]{1,0:T(8,128)(2,1)} copy(bf16[2048,128]{1,0:T(8,128)(2,1)} %bitcast.11) | data formatting | bytes 1048576
  121.6 1.9 %copy.16 = bf16[2048,128]{1,0:T(8,128)(2,1)} copy(bf16[2048,128]{1,0:T(8,128)(2,1)} %bitcast.10) | data formatting | bytes 1048576
  (14 shorter events, 0.1 us)
Async XLA Ops:
  2.0 13.3 %all-to-all-start = ((s32[32,1,1]{2,1,0:T(1,128)}), s32[32,1,1]{2,1,0:T(1,128)S(1)}, u32[]{:S(2)}, u32[]{:S(2)}) async-start(s32[32,1,1]{2,1,0:T(1,128)} %copy.11), calls=%async_computation | async-start | bytes 32768 | tf_op jit(solution)/shard_map/all_to_all | solution.py:226

commit v2 on v1

v2 whole, which is shorter than its diff:
```python
import functools

import jax
import jax.numpy as jnp
from jax import lax
from jax.experimental import pallas as pl
from jax.experimental.pallas import tpu as pltpu
from jax.sharding import PartitionSpec as P

ITERS = 2
UNROLL = 4
epsilon = 1e-06
MESH = pl.DeviceIdType.MESH


def lanes_for(count):
    return -(-count // 128) * 128


def index_along(shape, axis):
    return lax.broadcasted_iota(jnp.int32, shape, axis).astype(jnp.float32)


def place_groups(keys, groups, per_slot, slots, out, seat_row, last_row):
    items, lanes = keys.shape[1], lanes_for(groups)
    key = jnp.broadcast_to(keys, (items, items))
    key_down = jnp.broadcast_to(keys, (lanes_for(items), items)).T
    before = (key_down[:, :items] == key) & (
        index_along((items, items), 1) < index_along((items, items), 0)
    )
    rank = jnp.sum(before.astype(jnp.float32), axis=1, keepdims=True)
    lane = index_along((items, lanes), 1)
    member = (jnp.broadcast_to(key_down[:, :1], (items, lanes)) == lane).astype(jnp.float32)
    count = jnp.sum(member, axis=0, keepdims=True)
    used = jnp.floor((count + (per_slot - 1)) * (1.0 / per_slot))
    used_down = jnp.broadcast_to(used, (lanes, lanes)).T
    earlier = (index_along((lanes, lanes), 0) < index_along((lanes, lanes), 1)).astype(jnp.float32)
    start = jnp.sum(used_down * earlier, axis=0, keepdims=True)
    last = jnp.where(used > 0, start + used - 1, float(slots))
    first = jnp.sum(member * start, axis=1, keepdims=True)
    place = jnp.where(key_down[:, :1] >= 0, per_slot * first + rank, -1.0)
    seats = lanes_for(slots * per_slot)
    for chunk in range(seats // 128):
        hot = jnp.broadcast_to(place, (items, 128)) == index_along((items, 128), 1) + 128 * chunk
        item = jnp.where(hot, index_along((items, 128), 0) - items, 0.0)
        chosen = items + jnp.sum(item, axis=0, keepdims=True)
        out[pl.ds(seat_row + chunk, 1), :] = chosen.astype(jnp.int32)
    for chunk in range(lanes // 128):
        out[pl.ds(last_row + chunk, 1), :] = last[:, 128 * chunk : 128 * (chunk + 1)].astype(
            jnp.int32
        )


def slots_for(items, groups):
    pairs = (items + min(items, groups)) // 2
    return -(-pairs // UNROLL) * UNROLL


def kernel(
    n,
    f_slots,
    b_slots,
    row_of,
    peer_of,
    live_count,
    rows_lane,
    peers_lane,
    need,
    source,
    target_hbm,
    tiles_hbm,
    source_out,
    target_out,
    x_out,
    x_ins,
    y_out,
    y_ins,
    x_now,
    y_now,
    y_base,
    f_sums,
    b_sums,
    c_sums,
    target,
    tiles,
    need_all,
    need_at,
    tile_plan,
    tile_at,
    part_plan,
    part_at,
    send_sem,
    recv_sem,
    need_send,
    need_recv,
    load_sem,
):
    me = lax.axis_index("rows")
    rows, side, width = source.shape
    tile_total = tiles_hbm.shape[0]
    f_seat, f_last = 0, lanes_for(2 * f_slots) // 128
    b_seat = f_last + lanes_for(rows) // 128
    b_last = b_seat + lanes_for(2 * b_slots) // 128
    c_last = lanes_for(n) // 128

    barrier = pltpu.get_barrier_semaphore()

    def greet(k, carry):
        pl.semaphore_signal(
            barrier, inc=1, device_id=(lax.rem(me + k, n),), device_id_type=MESH
        )
        return carry

    lax.fori_loop(1, n, greet, 0)
    target_load = pltpu.make_async_copy(target_hbm, target, load_sem.at[0])
    target_load.start()
    tile_load = pltpu.make_async_copy(tiles_hbm, tiles.at[pl.ds(0, tile_total)], load_sem.at[1])
    tile_load.start()

    zero_block = jnp.zeros((side, width), jnp.bfloat16)
    zero_sum = jnp.zeros((side, width), jnp.float32)
    tiles[tile_total] = jnp.zeros((side, side), jnp.bfloat16)
    f_sums[f_slots] = zero_sum
    b_sums[b_slots] = zero_block
    c_sums[n] = zero_sum
    need_all[me] = need[...]
    pl.semaphore_wait(barrier, n - 1)

    def ask(k, carry):
        pltpu.make_async_remote_copy(
            src_ref=need,
            dst_ref=need_all.at[me],
            send_sem=need_send.at[0],
            recv_sem=need_recv.at[0],
            device_id=(lax.rem(me + k, n),),
            device_id_type=MESH,
        ).start()
        return carry

    lax.fori_loop(1, n, ask, 0)

    def turn(b, carry):
        flipped = target[b].astype(jnp.float32).T
        y_base[b] = flipped
        y_now[b] = flipped.astype(jnp.bfloat16)
        return carry

    def plan_tiles():
        live = lax.broadcasted_iota(jnp.int32, (1, tile_total), 1) < live_count[0]
        row_keys = jnp.where(live, rows_lane[...], -1).astype(jnp.float32)
        peer_keys = jnp.where(live, peers_lane[...], -1).astype(jnp.float32)
        place_groups(row_keys, rows, 2, f_slots, tile_plan, f_seat, f_last)
        place_groups(peer_keys, n, 2, b_slots, tile_plan, b_seat, b_last)
        load = pltpu.make_async_copy(tile_plan, tile_at, load_sem.at[3])
        load.start()
        load.wait()

    def plan_parts():
        table = need_all[...].reshape(n, need_all.shape[2]).astype(jnp.float32)
        mine = index_along(table.shape, 1) == me.astype(jnp.float32)
        wanted = jnp.sum(jnp.where(mine, table, 0.0), axis=1, keepdims=True)
        keys = jnp.broadcast_to(wanted, (n, 128)).T[:1]
        place_groups(keys, rows, 1, n, part_plan, 0, c_last)
        load = pltpu.make_async_copy(part_plan, part_at, load_sem.at[4])
        load.start()
        load.wait()

    def seat(table, first, index, top):
        return jnp.clip(table[first + index // 128, index % 128], 0, top)

    def tile_pair(first, q):
        left = seat(tile_at, first, 2 * q, tile_total)
        right = seat(tile_at, first, 2 * q + 1, tile_total)
        return left, right, jnp.minimum(left, tile_total - 1), jnp.minimum(right, tile_total - 1)

    def asked(d):
        return jnp.clip(need_at[d, 0, me], 0, rows - 1)

    def send(out, inn, phase, it, fill):
        def one(k, carry):
            peer = lax.rem(me + k, n)
            out[it, peer] = fill(peer)
            pltpu.make_async_remote_copy(
                src_ref=out.at[it, peer],
                dst_ref=inn.at[me],
                send_sem=send_sem.at[phase],
                recv_sem=recv_sem.at[phase],
                device_id=(peer,),
                device_id_type=MESH,
            ).start()
            return carry

        lax.fori_loop(1, n, one, 0)
        inn[me] = fill(me)

    def all_of(buffer, sem):
        view = buffer.at[pl.ds(0, n - 1)]
        pltpu.make_async_copy(view, view, sem).wait()

    def send_x(blocks, it):
        send(x_out, x_ins[it], 2 * it, it, lambda p: blocks[asked(p)])

    def backward(it):
        def one(q, carry):
            total, key = carry
            left, right, left_at, right_at = tile_pair(b_seat, q)
            flipped = jnp.concatenate([y_now[row_of[left_at]], y_now[row_of[right_at]]], axis=1)
            stack = jnp.concatenate([tiles[left], tiles[right]], axis=0)
            product = jnp.dot(flipped, stack, preferred_element_type=jnp.float32)
            new_key = peer_of[left_at]
            total = total * (new_key == key).astype(jnp.float32) + product
            b_sums[q] = total.astype(jnp.bfloat16)
            return total, new_key

        lax.fori_loop(0, b_slots, one, (zero_sum, jnp.int32(-1)), unroll=UNROLL)
        send(y_out, y_ins[it], 2 * it + 1, it, lambda p: b_sums[seat(tile_at, b_last, p, b_slots)])

    def forward(it, result):
        x_in = x_ins[it]
        all_of(x_in, recv_sem.at[2 * it])

        def one(q, carry):
            total, key = carry
            left, right, left_at, right_at = tile_pair(f_seat, q)
            stack = jnp.concatenate([tiles[left], tiles[right]], axis=1)
            blocks = jnp.concatenate([x_in[peer_of[left_at]], x_in[peer_of[right_at]]], axis=0)
            product = jnp.dot(stack, blocks, preferred_element_type=jnp.float32)
            new_key = row_of[left_at]
            total = total * (new_key == key).astype(jnp.float32) + product
            f_sums[q] = total
            return total, new_key

        lax.fori_loop(0, f_slots, one, (zero_sum, jnp.int32(-1)), unroll=UNROLL)

        def settle(b, carry):
            total = source[b].astype(jnp.float32) + f_sums[seat(tile_at, f_last, b, f_slots)]
            scale = lax.rsqrt(jnp.mean(total * total, axis=-1, keepdims=True) + epsilon)
            result[b] = (total * scale).astype(jnp.bfloat16)
            return carry

        lax.fori_loop(0, rows, settle, 0)

    def combine(it, final):
        y_in = y_ins[it]
        all_of(y_in, recv_sem.at[2 * it + 1])

        def one(k, carry):
            total, key = carry
            sender = seat(part_at, 0, k, n - 1)
            new_key = asked(sender)
            total = total * (new_key == key).astype(jnp.float32) + y_in[sender].astype(jnp.float32)
            c_sums[k] = total
            return total, new_key

        lax.fori_loop(0, n, one, (zero_sum, jnp.int32(-1)), unroll=UNROLL)

        def settle(b, carry):
            total = y_base[b] + c_sums[seat(part_at, c_last, b, n)]
            scale = lax.rsqrt(jnp.mean(total * total, axis=0, keepdims=True) + epsilon)
            if final:
                target_out[b] = (total * scale).T.astype(jnp.bfloat16)
            else:
                y_now[b] = (total * scale).astype(jnp.bfloat16)
            return carry

        lax.fori_loop(0, rows, settle, 0)

    all_of(need_all, need_recv.at[0])
    need_load = pltpu.make_async_copy(need_all, need_at, load_sem.at[2])
    need_load.start()
    need_load.wait()
    send_x(source, 0)
    plan_tiles()
    target_load.wait()
    lax.fori_loop(0, rows, turn, 0)
    tile_load.wait()
    backward(0)
    plan_parts()
    for it in range(ITERS):
        final = it == ITERS - 1
        forward(it, source_out if final else x_now)
        if not final:
            send_x(x_now, it + 1)
        combine(it, final)
        if not final:
            backward(it + 1)
    all_of(need_all, need_send.at[0])
    for it in range(ITERS):
        all_of(x_out.at[it], send_sem.at[2 * it])
        all_of(y_out.at[it], send_sem.at[2 * it + 1])


def shards(source, target, tile_values, tile_rows, tile_peers, need_list, tile_count):
    n = lax.axis_size("rows")
    tiles_here, side, _ = tile_values.shape
    width = source.shape[1]
    rows = source.shape[0] // side
    f_slots = slots_for(tiles_here, rows)
    b_slots = slots_for(tiles_here, n)
    tile_plan = (
        lanes_for(2 * f_slots) + lanes_for(rows) + lanes_for(2 * b_slots) + lanes_for(n)
    ) // 128
    part_plan = (lanes_for(n) + lanes_for(rows)) // 128
    wide = lanes_for(n)
    need = jnp.pad(need_list.reshape(1, n), ((0, 0), (0, wide - n)))
    block = (side, width)
    vmem = pl.BlockSpec(memory_space=pltpu.VMEM)
    smem = pl.BlockSpec(memory_space=pltpu.SMEM)
    source_now, target_now = pl.pallas_call(
        functools.partial(kernel, n, f_slots, b_slots),
        out_shape=[jax.ShapeDtypeStruct((rows,) + block, jnp.bfloat16)] * 2,
        in_specs=[smem] * 3 + [vmem] * 4 + [pl.BlockSpec(memory_space=pl.ANY)] * 2,
        out_specs=[vmem, vmem],
        scratch_shapes=[
            pltpu.VMEM((ITERS, n) + block, jnp.bfloat16),
            [pltpu.VMEM((n,) + block, jnp.bfloat16)] * ITERS,
            pltpu.VMEM((ITERS, n) + block, jnp.bfloat16),
            [pltpu.VMEM((n,) + block, jnp.bfloat16)] * ITERS,
            pltpu.VMEM((rows,) + block, jnp.bfloat16),
            pltpu.VMEM((rows,) + block, jnp.bfloat16),
            pltpu.VMEM((rows,) + block, jnp.float32),
            pltpu.VMEM((f_slots + 1,) + block, jnp.float32),
            pltpu.VMEM((b_slots + 1,) + block, jnp.bfloat16),
            pltpu.VMEM((n + 1,) + block, jnp.float32),
            pltpu.VMEM((rows,) + block, jnp.bfloat16),
            pltpu.VMEM((tiles_here + 1, side, side), jnp.bfloat16),
            pltpu.VMEM((n, 1, wide), jnp.int32),
            pltpu.SMEM((n, 1, wide), jnp.int32),
            pltpu.VMEM((tile_plan, 128), jnp.int32),
            pltpu.SMEM((tile_plan, 128), jnp.int32),
            pltpu.VMEM((part_plan, 128), jnp.int32),
            pltpu.SMEM((part_plan, 128), jnp.int32),
            pltpu.SemaphoreType.DMA((2 * ITERS,)),
            pltpu.SemaphoreType.DMA((2 * ITERS,)),
            pltpu.SemaphoreType.DMA((1,)),
            pltpu.SemaphoreType.DMA((1,)),
            pltpu.SemaphoreType.DMA((5,)),
        ],
        compiler_params=pltpu.CompilerParams(
            collective_id=0, has_side_effects=True, vmem_limit_bytes=67043328
        ),
    )(
        tile_rows,
        tile_peers,
        tile_count,
        tile_rows.reshape(1, -1),
        tile_peers.reshape(1, -1),
        need,
        source.reshape((rows,) + block),
        target.reshape((rows,) + block),
        tile_values,
    )
    return source_now.reshape(-1, width), target_now.reshape(-1, width)


def solution(mesh):
    return jax.shard_map(
        shards,
        mesh=mesh,
        in_specs=(
            P("rows", None),
            P("rows", None),
            P("rows", None, None),
            P("rows"),
            P("rows"),
            P("rows", None),
            P("rows"),
        ),
        out_specs=(P("rows", None), P("rows", None)),
        check_vma=False,
    )
```

time: 125 us -> 113 us (0.904)
  other arithmetic: 7.68 us -> 0 us
  starting transfers between devices: 6.27 us -> 0 us
  Pallas kernels: 102 us -> 106 us
    reduce_sum x14 -> x0, other arithmetic: 6.4 us -> none  [the longest x3 1.66 us: plan_groups(): count = jnp.sum(member.astype(jnp.int32), axis=1)]
    all_to_all x1 -> x0, starting transfers between devices: 6.27 us -> none  [shards(): lax.all_to_all(need_list.reshape(n, 1), 'rows', split_axis=0, concat_axis...]
    pallas_call x1, Pallas kernels: 102 us -> 106 us  [shards(): pl.pallas_call(functools.partial(kernel, n, f_slots, b_slots), out_shape=...]
    all_to_all x1 -> x0, local copies, waits for them, and re-layouts: 1.34 us -> none  [shards(): lax.all_to_all(need_list.reshape(n, 1), 'rows', split_axis=0, concat_axis...]
  transfers between devices with their start and end apart: 1 -> 0, of which waited for: 0 -> 0; matrix products, arithmetic and copies ran while one was open for 5% -> 0% of each run, Pallas kernels for 0% -> 0%
where the time goes in v2:
time: 113 us
  Pallas kernels  106 us (94%)
  local copies, waits for them, and re-layouts  4.91 us (4%)
  between operations  1.29 us (1%)
    pallas_call x1, Pallas kernels, shards(): pl.pallas_call(functools.partial(kernel, n, f_slots, b_slots), out_shape=...  106 us
    unnamed x2, local copies, waits for them, and re-layouts  3.74 us

profile of v2, /device:TPU:13, one launch (start us, length us, event | category | flops | bytes accessed | tf_op | source)
XLA Modules:
  0.0 112.7 jit_solution(17161391154110491208)
XLA Ops:
  1.3 1.2 %pad.4.need = s32[1,128]{1,0:T(1,128)} pad(s32[1,32]{1,0:T(1,128)} %param.12, s32[]{:T(128)} %constant.0.clone.1), padding=0_0x0_96 | pad | bytes 644 | tf_op jit(solution)/shard_map/jit(_pad)/pad | solution.py:305
  2.4 106.5 %shard_map.86 = (bf16[16,128,128]{2,1,0:T(8,128)(2,1)}, bf16[16,128,128]{2,1,0:T(8,128)(2,1)}) custom-call(s32[128]{0:T(128)} %row_of.1, s32[128]{0:T(128)} %peer_of.1, s32[1]{0:T(128)S(6)} %copy.11.live_count, s32[1,128]{1,0:T(1,128)} %bitcast.10, s32[1,128]{1,0:T(1,128)} %bitcast.11, s32[1,128]{1,0:T(1,128)} %pad.4.need, bf16[16,128,128]{2,1,0:T(8,128)(2,1)} %bitcast.8, ...), custom_call_target="tpu_custom_call" | custom-call | tf_op jit(solution)/shard_map/pallas_call | solution.py:309
  108.9 1.9 %copy.12 = bf16[2048,128]{1,0:T(8,128)(2,1)} copy(bf16[2048,128]{1,0:T(8,128)(2,1)} %bitcast.7) | data formatting | bytes 1048576
  110.8 1.9 %copy.13 = bf16[2048,128]{1,0:T(8,128)(2,1)} copy(bf16[2048,128]{1,0:T(8,128)(2,1)} %bitcast.6) | data formatting | bytes 1048576

commit v3 on v2

--- a/solution.py
+++ b/solution.py
@@ -66,7 +66,7 @@
     rows_lane,
     peers_lane,
     need,
-    source,
+    source_hbm,
     target_hbm,
     tiles_hbm,
     source_out,
@@ -81,6 +81,7 @@
     f_sums,
     b_sums,
     c_sums,
+    source,
     target,
     tiles,
     need_all,
@@ -112,6 +113,8 @@
         return carry
 
     lax.fori_loop(1, n, greet, 0)
+    source_load = pltpu.make_async_copy(source_hbm, source, load_sem.at[5])
+    source_load.start()
     target_load = pltpu.make_async_copy(target_hbm, target, load_sem.at[0])
     target_load.start()
     tile_load = pltpu.make_async_copy(tiles_hbm, tiles.at[pl.ds(0, tile_total)], load_sem.at[1])
@@ -269,6 +272,7 @@
     need_load = pltpu.make_async_copy(need_all, need_at, load_sem.at[2])
     need_load.start()
     need_load.wait()
+    source_load.wait()
     send_x(source, 0)
     plan_tiles()
     target_load.wait()
@@ -301,15 +305,13 @@
         lanes_for(2 * f_slots) + lanes_for(rows) + lanes_for(2 * b_slots) + lanes_for(n)
     ) // 128
     part_plan = (lanes_for(n) + lanes_for(rows)) // 128
-    wide = lanes_for(n)
-    need = jnp.pad(need_list.reshape(1, n), ((0, 0), (0, wide - n)))
     block = (side, width)
     vmem = pl.BlockSpec(memory_space=pltpu.VMEM)
     smem = pl.BlockSpec(memory_space=pltpu.SMEM)
     source_now, target_now = pl.pallas_call(
         functools.partial(kernel, n, f_slots, b_slots),
         out_shape=[jax.ShapeDtypeStruct((rows,) + block, jnp.bfloat16)] * 2,
-        in_specs=[smem] * 3 + [vmem] * 4 + [pl.BlockSpec(memory_space=pl.ANY)] * 2,
+        in_specs=[smem] * 3 + [vmem] * 3 + [pl.BlockSpec(memory_space=pltpu.HBM)] * 3,
         out_specs=[vmem, vmem],
         scratch_shapes=[
             pltpu.VMEM((ITERS, n) + block, jnp.bfloat16),
@@ -323,9 +325,10 @@
             pltpu.VMEM((b_slots + 1,) + block, jnp.bfloat16),
             pltpu.VMEM((n + 1,) + block, jnp.float32),
             pltpu.VMEM((rows,) + block, jnp.bfloat16),
+            pltpu.VMEM((rows,) + block, jnp.bfloat16),
             pltpu.VMEM((tiles_here + 1, side, side), jnp.bfloat16),
-            pltpu.VMEM((n, 1, wide), jnp.int32),
-            pltpu.SMEM((n, 1, wide), jnp.int32),
+            pltpu.VMEM((n, 1, n), jnp.int32),
+            pltpu.SMEM((n, 1, n), jnp.int32),
             pltpu.VMEM((tile_plan, 128), jnp.int32),
             pltpu.SMEM((tile_plan, 128), jnp.int32),
             pltpu.VMEM((part_plan, 128), jnp.int32),
@@ -334,7 +337,7 @@
             pltpu.SemaphoreType.DMA((2 * ITERS,)),
             pltpu.SemaphoreType.DMA((1,)),
             pltpu.SemaphoreType.DMA((1,)),
-            pltpu.SemaphoreType.DMA((5,)),
+            pltpu.SemaphoreType.DMA((6,)),
         ],
         compiler_params=pltpu.CompilerParams(
             collective_id=0, has_side_effects=True, vmem_limit_bytes=67043328
@@ -345,7 +348,7 @@
         tile_count,
         tile_rows.reshape(1, -1),
         tile_peers.reshape(1, -1),
-        need,
+        need_list,
         source.reshape((rows,) + block),
         target.reshape((rows,) + block),
         tile_values,

time: 113 us -> 111 us (0.982)
  local copies, waits for them, and re-layouts: 4.91 us -> 3.74 us
    pad x1 -> x0, local copies, waits for them, and re-layouts: 1.17 us -> none  [shards(): need = jnp.pad(need_list.reshape(1, n), ((0, 0), (0, wide - n)))]
where the time goes in v3:
time: 111 us
  Pallas kernels  106 us (95%)
  local copies, waits for them, and re-layouts  3.74 us (3%)
  between operations  1.29 us (1%)
    pallas_call x1, Pallas kernels, shards(): pl.pallas_call(functools.partial(kernel, n, f_slots, b_slots), out_shape=...  106 us
    unnamed x2, local copies, waits for them, and re-layouts  3.74 us

profile of v3, /device:TPU:13, one launch (start us, length us, event | category | flops | bytes accessed | tf_op | source)
XLA Modules:
  0.0 111.2 jit_solution(779150285730979547)
XLA Ops:
  1.3 106.2 %shard_map.86 = (bf16[16,128,128]{2,1,0:T(8,128)(2,1)}, bf16[16,128,128]{2,1,0:T(8,128)(2,1)}) custom-call(s32[128]{0:T(128)} %row_of.1, s32[128]{0:T(128)} %peer_of.1, s32[1]{0:T(128)S(6)} %copy.11.live_count, s32[1,128]{1,0:T(1,128)} %bitcast.10, s32[1,128]{1,0:T(1,128)} %bitcast.11, s32[1,32]{1,0:T(1,128)} %need.1, bf16[16,128,128]{2,1,0:T(8,128)(2,1)} %bitcast.8, ...), custom_call_target="tpu_custom_call" | custom-call | tf_op jit(solution)/shard_map/pallas_call | solution.py:311
  107.5 1.9 %copy.12 = bf16[2048,128]{1,0:T(8,128)(2,1)} copy(bf16[2048,128]{1,0:T(8,128)(2,1)} %bitcast.7) | data formatting | bytes 1048576
  109.4 1.9 %copy.13 = bf16[2048,128]{1,0:T(8,128)(2,1)} copy(bf16[2048,128]{1,0:T(8,128)(2,1)} %bitcast.6) | data formatting | bytes 1048576
